TPU v7x, 32 devices: a whole 2x2x4 slice. The times are simulated.
32 devices in a mesh: section: 2 (over x), expert: 4 (over y, core), dp: 4 (over z).
Axes of the slice: x: 2, y: 2, z: 4, core: 2. Of those that a mesh axis runs over, the one named last changes fastest.
Arguments:
- x_in: bfloat16 [8, 256, 2048], P(None, ('expert', 'dp'), 'section'), may hold values from -6 to 6
- cotangent: bfloat16 [8, 256, 2048], P(None, ('expert', 'dp'), 'section'), may hold values from -6 to 6
- route_ids: int32 [2, 8, 256, 2], P('section', None, ('expert', 'dp')), may hold values from 0 to 15, all different within a row; in each aligned block of 16 rows (0 to 15, 16 to 31, ..., all dimensions but the last counted through in order) at most 2 rows name the same one
- norm_gain: float32 [2, 2048], P('section'), may hold values from 0.5 to 1.5
- router: bfloat16 [2, 2048, 16], P('section'), may hold values from -0.125 to 0.125
- w_gate_up: bfloat16 [2, 16, 2048, 1024], P('section', ('expert', 'dp')), may hold values from -0.125 to 0.125
- w_down: bfloat16 [2, 16, 512, 2048], P('section', ('expert', 'dp')), may hold values from -0.25 to 0.25
Outputs:
- grad_in: bfloat16 [8, 256, 2048], P(None, ('expert', 'dp'), 'section')
- grad_gate_up: float32 [2, 16, 2048, 1024], P('section', ('expert', 'dp'))
- grad_down: float32 [2, 16, 512, 2048], P('section', ('expert', 'dp'))
- grad_router: float32 [2, 2048, 16], P('section')
- grad_gain: float32 [2, 2048], P('section')
Inputs may be any that keep to these rules, and one draw needn't show every extreme that they name: `route_ids`: each row names two different experts; the 16 rows of one device in one layer and micro-batch name any expert at most 2 times, a bound that some block reaches in some of them.
All inputs are finite; a program needn't handle non-finite values.
Results may differ from a plain program's by a relative error of at most 0.035.
Values may be sent and summed in bfloat16 or wider, within the bound.
A program may use at most 64 MiB of HBM per device.

v0:
```python
import functools

import jax
import jax.numpy as jnp
from jax import lax
from jax.experimental import pallas as pl
from jax.experimental.pallas import tpu as pltpu
from jax.sharding import PartitionSpec as P

EPS = 1e-05
CHUNKS = 2
LANES = 128
F32 = jnp.float32
BF16 = jnp.bfloat16


def exchange_body(n_arr, n_expert_axis, n_dp_axis, *refs):
    ins, outs = refs[:n_arr], refs[n_arr : 2 * n_arr]
    send_sem, recv_sem = refs[2 * n_arr :]
    n_rank = n_expert_axis * n_dp_axis
    me = lax.axis_index("expert") * n_dp_axis + lax.axis_index("dp")

    def place(step):
        rank = lax.rem(me + step, n_rank)
        return rank, {"expert": lax.div(rank, n_dp_axis), "dp": lax.rem(rank, n_dp_axis)}

    barrier = pltpu.get_barrier_semaphore()
    for step in range(1, n_rank):
        pl.semaphore_signal(
            barrier, inc=1, device_id=place(step)[1], device_id_type=pl.DeviceIdType.MESH
        )
    pl.semaphore_wait(barrier, n_rank - 1)
    copies = []
    for step in range(1, n_rank):
        rank, device = place(step)
        for i in range(n_arr):
            copy = pltpu.make_async_remote_copy(
                src_ref=ins[i].at[rank],
                dst_ref=outs[i].at[me],
                send_sem=send_sem.at[i, step],
                recv_sem=recv_sem.at[i, step],
                device_id=device,
                device_id_type=pl.DeviceIdType.MESH,
            )
            copy.start()
            copies.append(copy)
    for i in range(n_arr):
        outs[i][me] = ins[i][me]
    for copy in copies:
        copy.wait()


def exchange(arrays, collective_id):
    n_rank = arrays[0].shape[0]
    n_expert_axis, n_dp_axis = lax.axis_size("expert"), lax.axis_size("dp")
    spec = pl.BlockSpec(memory_space=pltpu.VMEM)
    return pl.pallas_call(
        functools.partial(exchange_body, len(arrays), n_expert_axis, n_dp_axis),
        out_shape=[jax.ShapeDtypeStruct(a.shape, a.dtype) for a in arrays],
        in_specs=[spec] * len(arrays),
        out_specs=[spec] * len(arrays),
        scratch_shapes=[
            pltpu.SemaphoreType.DMA((len(arrays), n_rank)),
            pltpu.SemaphoreType.DMA((len(arrays), n_rank)),
        ],
        compiler_params=pltpu.CompilerParams(
            collective_id=collective_id, has_side_effects=True
        ),
    )(*arrays)


def dot(a, b, dims, precision=None):
    return lax.dot_general(
        a, b, ((dims[:1], dims[1:]), ((), ())), precision=precision, preferred_element_type=F32
    )


def tick_body(cfg, in_names, out_names, *refs):
    n_in, n_out = len(in_names), len(out_names)
    r = dict(zip(in_names, refs[:n_in]))
    o = dict(zip(out_names, refs[n_in : n_in + n_out]))
    (gu_buf, dn_buf, sent_buf, land_buf, reply_buf, back_buf,
     side_out, side_land, side_reply, side_back,
     copy_sem, send_sem, recv_sem) = refs[n_in + n_out :]
    tick, chunks, last = cfg["tick"], cfg["chunks"], cfg["last"]
    any_f, any_t, any_b, seed = cfg["any_f"], cfg["any_t"], cfg["any_b"], cfg["seed"]
    n_dp, n_rank = cfg["n_dp"], cfg["n_rank"]
    cells, width = land_buf.shape
    block = cells // n_rank
    hidden_width = dn_buf.shape[0]
    tokens = cells // 2
    n_expert = n_rank
    section = lax.axis_index("section")
    me = lax.axis_index("expert") * n_dp + lax.axis_index("dp")

    def place(step):
        rank = lax.rem(me + step, n_rank)
        return rank, {"expert": lax.div(rank, n_dp), "dp": lax.rem(rank, n_dp)}

    load_gu = pltpu.make_async_copy(r["w_gu"], gu_buf, copy_sem.at[0])
    load_dn = pltpu.make_async_copy(r["w_dn"], dn_buf, copy_sem.at[1])
    load_gu.start()
    load_dn.start()
    barrier = pltpu.get_barrier_semaphore()
    for step in range(1, n_rank):
        pl.semaphore_signal(
            barrier, inc=1, device_id=place(step)[1], device_id_type=pl.DeviceIdType.MESH
        )

    def spread(phase, pairs):
        copies = []
        mine = pl.ds(pl.multiple_of(me * block, block), block)
        for step in range(1, n_rank):
            rank, device = place(step)
            theirs = pl.ds(pl.multiple_of(rank * block, block), block)
            for i, (a, b) in enumerate(pairs):
                copy = pltpu.make_async_remote_copy(
                    src_ref=a.at[theirs], dst_ref=b.at[mine],
                    send_sem=send_sem.at[phase, i, step], recv_sem=recv_sem.at[phase, i, step],
                    device_id=device, device_id_type=pl.DeviceIdType.MESH,
                )
                copy.start()
                copies.append(copy)
        for a, b in pairs:
            b[mine] = a[mine]
        for copy in copies:
            copy.wait()

    up, down = tick - section, tick - 2 * last + section
    is_top = section == last
    is_f = (up >= 0) & (up < chunks) & ~is_top
    is_t = (up >= 0) & (up < chunks) & is_top
    is_b = (down >= 0) & (down < chunks) & ~is_top
    index = jnp.clip(jnp.where(is_b, down, up), 0, chunks - 1)

    def choose(candidates):
        value = candidates[0][1]
        for flag, other in candidates[1:]:
            value = jnp.where(flag, other, value)
        return value

    h = choose([(f, r[k][...]) for f, k in
                ((None, "got_h"), (section == 0, "x"), (is_b, "prev_h")) if k in r])
    h_wide = h.astype(F32)
    inv = lax.rsqrt(jnp.mean(h_wide * h_wide, axis=-1, keepdims=True) + EPS)
    u = (h_wide * inv * r["gain"][...]).astype(BF16)
    across = r["cell_row"][index]
    downward = r["cell_col"][index]
    rows_iota = lax.broadcasted_iota(jnp.int32, (cells, tokens), 0)
    cols_iota = lax.broadcasted_iota(jnp.int32, (tokens, cells), 1)
    first = (across[0:1, :] == rows_iota).astype(F32)
    second = (across[1:2, :] == rows_iota).astype(F32)
    first_t = (downward[:, 0:1] == cols_iota).astype(F32)
    second_t = (downward[:, 1:2] == cols_iota).astype(F32)
    expert_iota = lax.broadcasted_iota(jnp.int32, (tokens, n_expert), 1) * block
    hit = [
        ((downward[:, k : k + 1] >= expert_iota) & (downward[:, k : k + 1] < expert_iota + block))
        .astype(F32)
        for k in range(2)
    ]
    logits = dot(u, r["router_t"][...], (1, 1))
    diff = jnp.sum((hit[0] - hit[1]) * logits, axis=1, keepdims=True)
    gate_1, gate_2 = jax.nn.sigmoid(diff), jax.nn.sigmoid(-diff)
    both = (first + second).astype(BF16)
    g_top = None
    if any_t or any_b:
        g_top = choose([(f, r[k][...]) for f, k in
                        ((None, "top"), (is_b, "got_g")) if k in r])
    source = u if (any_f or any_t) else g_top
    if any_b and (any_f or any_t):
        source = jnp.where(is_b, g_top, source)
    if seed:
        source = jnp.where(is_top, r["cot_0"][...], source)
    sent_buf[...] = dot(both, source, (1, 0)).astype(BF16)
    side_out[...] = dot(
        first, jnp.broadcast_to(gate_1, (tokens, LANES)), (1, 0), lax.Precision.HIGHEST
    ) + dot(second, jnp.broadcast_to(gate_2, (tokens, LANES)), (1, 0), lax.Precision.HIGHEST)
    pl.semaphore_wait(barrier, n_rank - 1)
    if any_f or any_t:
        spread(0, [(sent_buf, land_buf), (side_out, side_land)])
    else:
        spread(0, [(sent_buf, land_buf)])

    landed = land_buf[...]
    if "top_0" in o:
        o["top_0"][...] = landed
    if any_f or any_t:
        rows, gate_all = landed, side_land[...]
        if any_b:
            rows = jnp.where(is_b, r["prev_rows"][...], rows)
            gate_all = jnp.where(is_b, r["prev_gate"][...], gate_all)
        top_rows = r["top_rows"][...] if any_t else None
        if any_b:
            top_rows = jnp.where(is_b, landed, top_rows)
    else:
        rows, gate_all, top_rows = r["prev_rows"][...], r["prev_gate"][...], landed
    gate_here = gate_all[:, :1]
    if "h" in o:
        o["h"][...] = h
        o["gate"][...] = gate_all
    o["rows"][...] = rows
    load_gu.wait()
    load_dn.wait()
    gate_up = dot(rows, gu_buf[...], (1, 0))
    a, b = gate_up[:, :hidden_width], gate_up[:, hidden_width:]
    sig = jax.nn.sigmoid(a)
    hidden_f = a * sig * b
    hidden = hidden_f.astype(BF16)
    reply = None
    if any_f:
        reply = dot(hidden, dn_buf[...], (1, 0)).astype(BF16)
    if any_t or any_b:
        plain = dot(top_rows, dn_buf[...], (1, 1))
        c_col = jnp.sum(plain * hidden.astype(F32), axis=1, keepdims=True)
        side_reply[...] = jnp.broadcast_to(c_col, (cells, LANES))
        d_hidden = plain * gate_here
        slope = sig * (1.0 + a * (1.0 - sig))
        q = jnp.concatenate([d_hidden * b * slope, d_hidden * (a * sig)], axis=1).astype(BF16)
        o["q"][...] = q
        o["hidden"][...] = hidden
        o["dy"][...] = (top_rows.astype(F32) * gate_here).astype(BF16)
        du_rows = dot(q, gu_buf[...], (1, 1)).astype(BF16)
        reply = jnp.where(is_f, reply, du_rows) if any_f else du_rows
    if "top_1" in o:
        ahead = (
            (r["cell_row"][1][0:1, :] == rows_iota) | (r["cell_row"][1][1:2, :] == rows_iota)
        ).astype(F32).astype(BF16)
        reply = jnp.where(is_top, dot(ahead, r["cot_1"][...], (1, 0)).astype(BF16), reply)
    reply_buf[...] = reply
    if any_t or any_b:
        spread(1, [(reply_buf, back_buf), (side_reply, side_back)])
    else:
        spread(1, [(reply_buf, back_buf)])
    back = back_buf[...]
    if "top_1" in o:
        o["top_1"][...] = back
    picked_1 = dot(first_t.astype(BF16), back, (1, 0))
    picked_2 = dot(second_t.astype(BF16), back, (1, 0))
    if any_f:
        o["h_next"][...] = (h_wide + gate_1 * picked_1 + gate_2 * picked_2).astype(BF16)
    if any_t or any_b:
        c_diff = dot(first_t - second_t, side_back[...], (1, 0), lax.Precision.HIGHEST)[:, :1]
        cols = gate_1 * gate_2 * c_diff * (hit[0] - hit[1])
        du = picked_1 + picked_2 + dot(
            cols, r["router_t"][...].astype(F32), (1, 0), lax.Precision.HIGHEST
        )
        mine = is_t | is_b
        term = dot(cols, u.astype(F32), (0, 0), lax.Precision.HIGHEST)
        gain_term = jnp.sum(du * h_wide * inv, axis=0, keepdims=True)
        o["acc"][:n_expert, :] = jnp.where(mine, term, 0.0)
        o["acc"][n_expert:, :] = jnp.where(
            mine, jnp.broadcast_to(gain_term, (o["acc"].shape[0] - n_expert, width)), 0.0
        )
        scaled = du * r["gain"][...]
        projection = jnp.mean(scaled * h_wide, axis=-1, keepdims=True)
        o["g_out"][...] = (
            g_top.astype(F32) + inv * scaled - h_wide * (inv * inv * inv) * projection
        ).astype(BF16)


def tick_call(cfg, args, outs, number):
    w_gu = args["w_gu"]
    hidden_width, width = args["w_dn"].shape
    cells, n_rank = cfg["cells"], cfg["n_rank"]
    vmem = pl.BlockSpec(memory_space=pltpu.VMEM)
    hbm = pl.BlockSpec(memory_space=pl.ANY)
    names, out_names = list(args), list(outs)
    result = pl.pallas_call(
        functools.partial(tick_body, cfg, names, out_names),
        out_shape=[jax.ShapeDtypeStruct(*outs[k]) for k in out_names],
        in_specs=[hbm if k in ("w_gu", "w_dn") else vmem for k in names],
        out_specs=[vmem] * len(out_names),
        scratch_shapes=[pltpu.VMEM(w_gu.shape, BF16), pltpu.VMEM((hidden_width, width), BF16)]
        + [pltpu.VMEM((cells, width), BF16)] * 4
        + [pltpu.VMEM((cells, LANES), F32)] * 4
        + [pltpu.SemaphoreType.DMA((2,))]
        + [pltpu.SemaphoreType.DMA((2, 2, n_rank))] * 2,
        compiler_params=pltpu.CompilerParams(
            collective_id=number, has_side_effects=True, vmem_limit_bytes=48 * 1024 * 1024
        ),
    )(*[args[k] for k in names])
    return dict(zip(out_names, result))


def place_cells(route_all, n_expert, capacity, chunks):
    micro, tok, _ = route_all.shape
    per = micro // chunks
    hits = (route_all[..., None] == jnp.arange(n_expert, dtype=jnp.int32)).astype(jnp.int32)
    named = jnp.sum(hits, axis=2)
    earlier = (jnp.arange(tok)[:, None] > jnp.arange(tok)[None, :]).astype(jnp.int32)
    before = jnp.sum(earlier[None, :, :, None] * named[:, None, :, :], axis=2)
    slot = jnp.sum(hits * before[:, :, None, :], axis=3)
    within = (jnp.arange(micro, dtype=jnp.int32) % per)[:, None, None]
    cell = route_all * (per * capacity) + within * capacity + slot
    return cell.reshape(chunks, per * tok, 2)


def ends_gather(x_in, cotangent, section, n_section):
    if n_section == 1:
        return x_in, cotangent
    x_parts, top_parts = [], []
    last = n_section - 1
    for source in range(n_section):
        if source == 0:
            x_parts.append(x_in)
            continue
        other = last - source
        if other != source:
            got = lax.ppermute(
                jnp.where(section == source, x_in, cotangent),
                "section",
                [(source, 0), (other, last)],
            )
            x_parts.append(got)
            top_parts.append(got)
        else:
            x_parts.append(lax.ppermute(x_in, "section", [(source, 0)]))
            top_parts.append(lax.ppermute(cotangent, "section", [(other, last)]))
    top_parts = top_parts[::-1] + [cotangent]
    return jnp.concatenate(x_parts, axis=2), jnp.concatenate(top_parts, axis=2)


def local(x_in, cotangent, route_ids, norm_gain, router, w_gate_up, w_down):
    micro, tok, _ = x_in.shape
    n_section = lax.axis_size("section")
    n_rank = lax.axis_size("expert") * lax.axis_size("dp")
    per_rank, hidden_width, width = w_down.shape[1:]
    assert per_rank == 1
    n_expert = n_rank
    capacity = tok * 2 * 9 // (8 * n_expert)
    section = lax.axis_index("section")
    last = n_section - 1
    chunks = CHUNKS if n_section > 1 and micro % CHUNKS == 0 else 1
    per = micro // chunks
    tokens = per * tok
    block = per * capacity
    cells = n_rank * block
    gain = norm_gain[0]
    router_mat = router[0]
    w_gu, w_dn = w_gate_up[0, 0], w_down[0, 0]

    x_all, top_all = ends_gather(x_in, cotangent, section, n_section)
    x_all = x_all.reshape(chunks, tokens, width)
    top_all = top_all.reshape(chunks, tokens, width)
    cell_col = place_cells(route_ids[0], n_expert, capacity, chunks)
    cell_row = jnp.transpose(cell_col, (0, 2, 1))
    router_t = router_mat.T
    high = -(-(n_expert + 1) // 8) * 8
    assert n_section > 1
    token_rows, cell_rows = ((tokens, width), BF16), ((cells, width), BF16)
    ticks = chunks + 2 * last
    made = []
    got_h = got_g = None

    def by_section(values):
        result = values[0][1]
        for s, value in values[1:]:
            result = jnp.where(section == s, value, result)
        return result

    for tick in range(ticks):
        cfg = dict(
            tick=tick, chunks=chunks, last=last, cells=cells, n_rank=n_rank,
            n_dp=lax.axis_size("dp"), seed=tick == 0,
            any_f=any(0 <= tick - s < chunks for s in range(last)),
            any_t=0 <= tick - last < chunks,
            any_b=any(0 <= tick - 2 * last + s < chunks for s in range(last)),
        )
        args = dict(gain=gain[None], router_t=router_t, cell_row=cell_row, cell_col=cell_col)
        outs = dict(rows=cell_rows)
        if cfg["any_t"] or any(0 <= tick - s < chunks for s in range(1, last)):
            args["got_h"] = got_h
        if tick < chunks:
            args["x"] = x_all[tick]
        if cfg["any_t"]:
            args["top"] = top_all[tick - last]
            args["top_rows"] = made[0]["top_%d" % (tick - last)]
        if cfg["any_b"]:
            back_to = [
                (s, made[tick - 2 * last + 2 * s])
                for s in range(last)
                if 0 <= tick - 2 * last + s < chunks
            ]
            for key in ("h", "rows", "gate"):
                args["prev_" + key] = by_section([(s, state[key]) for s, state in back_to])
            args["got_g"] = got_g
        if tick == 0:
            for c in range(chunks):
                args["cot_%d" % c] = top_all[c]
                outs["top_%d" % c] = cell_rows
        if cfg["any_f"] or cfg["any_t"]:
            outs.update(h=token_rows, gate=((cells, LANES), F32))
        if cfg["any_f"]:
            outs["h_next"] = token_rows
        if cfg["any_t"] or cfg["any_b"]:
            outs.update(
                q=((cells, 2 * hidden_width), BF16), hidden=((cells, hidden_width), BF16),
                dy=cell_rows, g_out=token_rows, acc=((high, width), F32),
            )
        args["w_gu"], args["w_dn"] = w_gu, w_dn
        state = tick_call(cfg, args, outs, 2 + tick)
        made.append(state)
        if cfg["any_f"]:
            got_h = lax.ppermute(state["h_next"], "section", [(s, s + 1) for s in range(last)])
        if (cfg["any_t"] or cfg["any_b"]) and tick < ticks - 1:
            got_g = lax.ppermute(
                state["g_out"], "section", [(s, s - 1) for s in range(1, n_section)]
            )

    def finished(key):
        return jnp.concatenate(
            [
                by_section([(s, made[2 * last - s + c][key]) for s in range(n_section)])
                for c in range(chunks)
            ],
            axis=0,
        )

    grad_gu = dot(finished("rows"), finished("q"), (0, 0))
    grad_dn = dot(finished("hidden"), finished("dy"), (0, 0))
    acc = made[last]["acc"]
    for state in made[last + 1 :]:
        acc = acc + state["acc"]
    stash_out = jnp.stack([made[2 * last + c]["g_out"] for c in range(chunks)])

    piece = width // n_rank
    parts = jnp.transpose(acc.reshape(high, n_rank, piece), (1, 0, 2))
    (parts,) = exchange([parts], 1)
    total = jnp.broadcast_to(jnp.sum(parts, axis=0)[None], parts.shape)
    (total,) = exchange([total], 1)
    total = jnp.transpose(total, (1, 0, 2)).reshape(high, width)
    grad_router, grad_gain = total[:n_expert].T, total[n_expert]

    out = stash_out.reshape(micro, tok, n_section, width // n_section)
    grad_in = out[:, :, 0]
    for s in range(1, n_section):
        moved = lax.ppermute(out[:, :, s], "section", [(0, s)])
        grad_in = jnp.where(section == s, moved, grad_in)
    return (grad_in, grad_gu[None, None], grad_dn[None, None], grad_router[None], grad_gain[None])


def solution(mesh):
    in_specs = (
        P(None, ("expert", "dp"), "section"),
        P(None, ("expert", "dp"), "section"),
        P("section", None, ("expert", "dp"), None),
        P("section", None),
        P("section", None, None),
        P("section", ("expert", "dp"), None, None),
        P("section", ("expert", "dp"), None, None),
    )
    out_specs = (
        P(None, ("expert", "dp"), "section"),
        P("section", ("expert", "dp"), None, None),
        P("section", ("expert", "dp"), None, None),
        P("section", None, None),
        P("section", None),
    )
    return jax.shard_map(local, mesh=mesh, in_specs=in_specs, out_specs=out_specs, check_vma=False)
```

profile of v0, /device:TPU:0, one launch (start us, length us, event | category | flops | bytes accessed | tf_op | source)
XLA Modules:
  0.0 237.2 jit_solution(6871084128298127103)
XLA Ops:
  0.6 0.0 copy-start.16
  0.6 1.8 broadcast_select_fusion.6
  2.5 2.9 %collective-permute-start = (bf16[8,16,1024]{2,1,0:T(8,128)(2,1)}, bf16[8,16,1024]{2,1,0:T(8,128)(2,1)S(1)}, u32[]{:S(2)}, u32[]{:S(2)}) collective-permute-start(bf16[8,16,1024]{2,1,0:T(8,128)(2,1)} %get-tuple-element.73), channel_id=1, source_target_pairs={{16,0},{0,16},{17,1},{1,17},{18,2},{2,18},{19,3},{3,19},{20,4},{4,... | collective-permute-start | bytes 786440 | tf_op jit(solution)/shard_map/ppermute | solution.py:309
  5.4 0.7 broadcast_multiply_fusion
  6.1 0.8 convert_reduce_fusion
  6.9 0.3 multiply_reduce_fusion
  7.2 1.1 select_reduce_fusion
  8.4 0.1 add.35
  8.4 0.1 add.36
  8.5 0.1 copy.30
  8.6 0.1 copy.31
  8.8 0.1 bitcast_add_fusion.refs_3_
  8.9 0.1 copy.34.refs_2_
  8.9 3.0 %collective-permute-done = bf16[8,16,1024]{2,1,0:T(8,128)(2,1)S(1)} collective-permute-done((bf16[8,16,1024]{2,1,0:T(8,128)(2,1)}, bf16[8,16,1024]{2,1,0:T(8,128)(2,1)S(1)}, u32[]{:S(2)}, u32[]{:S(2)}) %collective-permute-start) | collective-permute-done | bytes 262176 | tf_op jit(solution)/shard_map/ppermute | solution.py:309
  11.9 0.7 copy-done.17
  12.6 1.0 constant_dynamic-update-slice_fusion.3
  13.6 0.0 copy-done.16
  13.7 0.0 copy-done
  13.7 0.0 copy-done.2
  13.8 0.0 copy-done.15
  13.8 34.6 %shard_map.110 = (bf16[128,2048]{1,0:T(8,128)(2,1)S(1)}, bf16[128,2048]{1,0:T(8,128)(2,1)S(1)}, bf16[128,2048]{1,0:T(8,128)(2,1)S(1)}, bf16[64,2048]{1,0:T(8,128...) custom-call(f32[1,2048]{1,0:T(1,128)S(1)} %copy-done.15, bf16[16,2048]{1,0:T(8,128)(2,1)S(1)} %bitcast.56, ...), custom_call_target="tpu_custom_call" | custom-call | tf_op jit(solution)/shard_map/pallas_call | solution.py:268
  48.4 3.3 %collective-permute-start.1 = (bf16[64,2048]{1,0:T(8,128)(2,1)S(1)}, bf16[64,2048]{1,0:T(8,128)(2,1)S(1)}, u32[]{:S(2)}, u32[]{:S(2)}) collective-permute-start(bf16[64,2048]{1,0:T(8,128)(2,1)S(1)} %get-tuple-element.32), channel_id=1, source_target_pairs={{0,16},{1,17},{2,18},{3,19},{4,20},{5,21},{6,22},{7,23},{8,24},{9,... | collective-permute-start | bytes 786440 | tf_op jit(solution)/shard_map/ppermute | solution.py:404
  51.7 5.8 %collective-permute-done.1.refs_4_ = bf16[64,2048]{1,0:T(8,128)(2,1)S(1)} collective-permute-done((bf16[64,2048]{1,0:T(8,128)(2,1)S(1)}, bf16[64,2048]{1,0:T(8,128)(2,1)S(1)}, u32[]{:S(2)}, u32[]{:S(2)}) %collective-permute-start.1) | collective-permute-done | bytes 262176 | tf_op jit(solution)/shard_map/ppermute | solution.py:404
  57.5 37.0 %shard_map.111 = (bf16[128,2048]{1,0:T(8,128)(2,1)S(1)}, bf16[64,2048]{1,0:T(8,128)(2,1)S(1)}, f32[128,128]{1,0:T(8,128)S(1)}, bf16[64,2048]{1,0:T(8,128)(2,1)S(...) custom-call(f32[1,2048]{1,0:T(1,128)S(1)} %copy-done.15, ...), custom_call_target="tpu_custom_call" | custom-call | tf_op jit(solution)/shard_map/pallas_call | solution.py:268
  94.6 0.0 copy-start.9
  94.6 0.6 copy-done.9
  95.2 4.4 %collective-permute-start.2 = (bf16[64,2048]{1,0:T(8,128)(2,1)S(1)}, bf16[64,2048]{1,0:T(8,128)(2,1)S(1)}, u32[]{:S(2)}, u32[]{:S(2)}) collective-permute-start(bf16[64,2048]{1,0:T(8,128)(2,1)S(1)} %get-tuple-element.34), channel_id=1, source_target_pairs={{0,16},{1,17},{2,18},{3,19},{4,20},{5,21},{6,22},{7,23},{8,24},{9,... | collective-permute-start | bytes 786440 | tf_op jit(solution)/shard_map/ppermute | solution.py:404
  99.6 1.5 collective-permute-start.3
  101.1 4.3 %collective-permute-done.2.refs_4_ = bf16[64,2048]{1,0:T(8,128)(2,1)S(1)} collective-permute-done((bf16[64,2048]{1,0:T(8,128)(2,1)S(1)}, bf16[64,2048]{1,0:T(8,128)(2,1)S(1)}, u32[]{:S(2)}, u32[]{:S(2)}) %collective-permute-start.2) | collective-permute-done | bytes 262176 | tf_op jit(solution)/shard_map/ppermute | solution.py:404
  105.4 4.1 %collective-permute-done.3.refs_10_ = bf16[64,2048]{1,0:T(8,128)(2,1)S(1)} collective-permute-done((bf16[64,2048]{1,0:T(8,128)(2,1)S(1)}, bf16[64,2048]{1,0:T(8,128)(2,1)S(1)}, u32[]{:S(2)}, u32[]{:S(2)}) %collective-permute-start.3) | collective-permute-done | bytes 262176 | tf_op jit(solution)/shard_map/ppermute | solution.py:406
  109.5 36.3 %shard_map.112 = (bf16[128,2048]{1,0:T(8,128)(2,1)S(1)}, bf16[64,2048]{1,0:T(8,128)(2,1)}, f32[128,128]{1,0:T(8,128)}, bf16[128,1024]{1,0:T(8,128)(2,1)S(1)}, bf...) custom-call(f32[1,2048]{1,0:T(1,128)S(1)} %copy-done.15, ...), custom_call_target="tpu_custom_call" | custom-call | tf_op jit(solution)/shard_map/pallas_call | solution.py:268
  145.8 0.0 copy-start.3
  145.9 0.7 copy-done.3
  146.6 1.3 collective-permute-start.4
  147.9 9.3 %collective-permute-done.4.refs_7_ = bf16[64,2048]{1,0:T(8,128)(2,1)S(1)} collective-permute-done((bf16[64,2048]{1,0:T(8,128)(2,1)S(1)}, bf16[64,2048]{1,0:T(8,128)(2,1)S(1)}, u32[]{:S(2)}, u32[]{:S(2)}) %collective-permute-start.4) | collective-permute-done | bytes 262176 | tf_op jit(solution)/shard_map/ppermute | solution.py:406
  157.1 0.0 copy-done.1
  157.1 34.5 %shard_map.113 = (bf16[128,2048]{1,0:T(8,128)(2,1)S(1)}, bf16[128,1024]{1,0:T(8,128)(2,1)S(1)}, bf16[128,512]{1,0:T(8,128)(2,1)S(1)}, bf16[128,2048]{1,0:T(8,128...) custom-call(f32[1,2048]{1,0:T(1,128)S(1)} %copy-done.15, bf16[16,2048]{1,0:T(8,128)(2,1)S(1)} %bitcast.59, ...), custom_call_target="tpu_custom_call" | custom-call | tf_op jit(solution)/shard_map/pallas_call | solution.py:268
  191.6 0.0 copy-done.7
  191.6 0.7 copy-done.5
  192.3 0.7 copy-done.8
  193.0 0.7 copy-done.13
  193.7 0.7 bitcast_bitcast_fusion.refs_0_
  194.4 10.5 %shard_map.114 = f32[16,24,128]{2,1,0:T(8,128)} custom-call(f32[16,24,128]{2,1,0:T(8,128)} %bitcast_bitcast_fusion.refs_0_), custom_call_target="tpu_custom_call" | custom-call | tf_op jit(solution)/shard_map/pallas_call | solution.py:57
  204.9 1.0 reduce_sum.42
  205.9 0.7 broadcast_in_dim.10.refs_0_
  206.6 10.3 %shard_map.115 = f32[16,24,128]{2,1,0:T(8,128)} custom-call(f32[16,24,128]{2,1,0:T(8,128)} %broadcast_in_dim.10.refs_0_), custom_call_target="tpu_custom_call" | custom-call | tf_op jit(solution)/shard_map/pallas_call | solution.py:57
  216.8 1.4 slice_bitcast_fusion.1
  218.3 1.6 bitcast_bitcast_fusion.1
  219.9 1.9 pad_maximum_fusion
  221.7 2.2 reshape.67
  223.9 2.3 fusion.17
  226.2 0.1 copy.50
  226.3 1.5 collective-permute-start.5
  227.8 0.1 broadcast_select_fusion.5
  227.9 0.0 copy-start.12
  227.9 0.0 copy-start.14
  227.9 0.2 broadcast_select_fusion.1
  228.1 0.6 copy-done.10
  228.8 0.1 copy-done.12
  228.8 0.1 copy-done.14
  228.9 2.8 %convolution_bitcast_fusion.1 = f32[1,1,512,2048]{3,2,1,0:T(8,128)} fusion(bf16[128,2048]{1,0:T(8,128)(2,1)S(1)} %get-tuple-element.60, bf16[128,2048]{1,0:T(8,128)(2,1)S(1)} %get-tuple-element.59, bf16[128,512]{1,0:T(8,128)(2,1)S(1)} %get-tuple-element.76, bf16[128,512]{1,0:T(8,128)(2,1)S(1)} %get-tuple-element.75), kind=kOutput, calls=%fused_computation.1 | convolution fusion | flops 539492352 | bytes 5505024 | tf_op jit(solution)/shard_map/dot_general | solution.py:73
  231.7 4.7 %convolution_bitcast_fusion = f32[1,1,2048,1024]{3,2,1,0:T(8,128)} fusion(bf16[128,2048]{1,0:T(8,128)(2,1)S(1)} %get-tuple-element.77, bf16[128,2048]{1,0:T(8,128)(2,1)S(1)} %get-tuple-element.78, bf16[128,1024]{1,0:T(8,128)(2,1)S(1)} %get-tuple-element.70, bf16[128,1024]{1,0:T(8,128)(2,1)S(1)} %get-tuple-element.69), kind=kOutput, calls=%fused_computation | convolution fusion | flops 1076887552 | bytes 9961472 | tf_op jit(solution)/shard_map/dot_general | solution.py:73
  236.4 0.0 collective-permute-done.5
  236.4 0.8 fusion.12
  (22 shorter events, 0.2 us)
Async XLA Ops:
  0.6 13.0 %copy-start.16 = (bf16[8,16,1024]{2,1,0:T(8,128)(2,1)S(1)}, bf16[8,16,1024]{2,1,0:T(8,128)(2,1)}, u32[]{:S(2)}) copy-start(bf16[8,16,1024]{2,1,0:T(8,128)(2,1)} %param.8) | copy-start | bytes 786436
  2.5 11.2 %copy-start = (bf16[1,1,512,2048]{3,2,1,0:T(8,128)(2,1)S(1)}, bf16[1,1,512,2048]{3,2,1,0:T(8,128)(2,1)}, u32[]{:S(2)}) copy-start(bf16[1,1,512,2048]{3,2,1,0:T(8,128)(2,1)} %param.13) | copy-start | bytes 6291460
  2.5 11.3 %copy-start.2 = (bf16[1,2048,16]{1,2,0:T(8,128)(2,1)S(1)}, bf16[1,2048,16]{1,2,0:T(8,128)(2,1)}, u32[]{:S(2)}) copy-start(bf16[1,2048,16]{1,2,0:T(8,128)(2,1)} %param.11) | copy-start | bytes 196612
  2.5 11.3 %copy-start.15 = (f32[1,2048]{1,0:T(1,128)S(1)}, f32[1,2048]{1,0:T(1,128)}, u32[]{:S(2)}) copy-start(f32[1,2048]{1,0:T(1,128)} %refs_0_.7) | copy-start | bytes 24580
  2.5 9.4 %collective-permute-start = (bf16[8,16,1024]{2,1,0:T(8,128)(2,1)}, bf16[8,16,1024]{2,1,0:T(8,128)(2,1)S(1)}, u32[]{:S(2)}, u32[]{:S(2)}) collective-permute-start(bf16[8,16,1024]{2,1,0:T(8,128)(2,1)} %get-tuple-element.73), channel_id=1, source_target_pairs={{16,0},{0,16},{17,1},{1,17},{18,2},{2,18},{19,3},{3,19},{20,4},{4,... | collective-permute-start | bytes 786440 | tf_op jit(solution)/shard_map/ppermute | solution.py:309
  11.9 0.7 copy-start.17
  48.4 9.1 %collective-permute-start.1 = (bf16[64,2048]{1,0:T(8,128)(2,1)S(1)}, bf16[64,2048]{1,0:T(8,128)(2,1)S(1)}, u32[]{:S(2)}, u32[]{:S(2)}) collective-permute-start(bf16[64,2048]{1,0:T(8,128)(2,1)S(1)} %get-tuple-element.32), channel_id=1, source_target_pairs={{0,16},{1,17},{2,18},{3,19},{4,20},{5,21},{6,22},{7,23},{8,24},{9,... | collective-permute-start | bytes 786440 | tf_op jit(solution)/shard_map/ppermute | solution.py:404
  94.6 0.6 copy-start.9
  95.2 10.2 %collective-permute-start.2 = (bf16[64,2048]{1,0:T(8,128)(2,1)S(1)}, bf16[64,2048]{1,0:T(8,128)(2,1)S(1)}, u32[]{:S(2)}, u32[]{:S(2)}) collective-permute-start(bf16[64,2048]{1,0:T(8,128)(2,1)S(1)} %get-tuple-element.34), channel_id=1, source_target_pairs={{0,16},{1,17},{2,18},{3,19},{4,20},{5,21},{6,22},{7,23},{8,24},{9,... | collective-permute-start | bytes 786440 | tf_op jit(solution)/shard_map/ppermute | solution.py:404
  99.6 9.9 %collective-permute-start.3 = (bf16[64,2048]{1,0:T(8,128)(2,1)S(1)}, bf16[64,2048]{1,0:T(8,128)(2,1)S(1)}, u32[]{:S(2)}, u32[]{:S(2)}) collective-permute-start(bf16[64,2048]{1,0:T(8,128)(2,1)S(1)} %get-tuple-element.39), channel_id=1, source_target_pairs={{16,0},{17,1},{18,2},{19,3},{20,4},{21,5},{22,6},{23,7},{24,8},{25... | collective-permute-start | bytes 786440 | tf_op jit(solution)/shard_map/ppermute | solution.py:406
  109.5 47.6 %copy-start.1 = (bf16[1,1,512,2048]{3,2,1,0:T(8,128)(2,1)S(1)}, bf16[1,1,512,2048]{3,2,1,0:T(8,128)(2,1)}, u32[]{:S(2)}) copy-start(bf16[1,1,512,2048]{3,2,1,0:T(8,128)(2,1)} %param.13) | copy-start | bytes 6291460
  145.8 0.7 copy-start.3
  146.6 45.0 %copy-start.7 = (bf16[64,2048]{1,0:T(8,128)(2,1)}, bf16[64,2048]{1,0:T(8,128)(2,1)S(1)}, u32[]{:S(2)}) copy-start(bf16[64,2048]{1,0:T(8,128)(2,1)S(1)} %get-tuple-element.40) | copy-start | bytes 786436
  146.6 45.1 %copy-start.11 = (bf16[128,512]{1,0:T(8,128)(2,1)}, bf16[128,512]{1,0:T(8,128)(2,1)S(1)}, u32[]{:S(2)}) copy-start(bf16[128,512]{1,0:T(8,128)(2,1)S(1)} %get-tuple-element.51) | copy-start | bytes 393220
  146.6 10.5 %collective-permute-start.4 = (bf16[64,2048]{1,0:T(8,128)(2,1)S(1)}, bf16[64,2048]{1,0:T(8,128)(2,1)S(1)}, u32[]{:S(2)}, u32[]{:S(2)}) collective-permute-start(bf16[64,2048]{1,0:T(8,128)(2,1)S(1)} %get-tuple-element.40), channel_id=1, source_target_pairs={{16,0},{17,1},{18,2},{19,3},{20,4},{21,5},{22,6},{23,7},{24,8},{25... | collective-permute-start | bytes 786440 | tf_op jit(solution)/shard_map/ppermute | solution.py:406
  191.6 0.7 copy-start.5
  192.3 0.7 copy-start.8
  193.0 0.7 copy-start.13
  223.9 3.8 %copy-start.4 = (bf16[128,1024]{1,0:T(8,128)(2,1)S(1)}, bf16[128,1024]{1,0:T(8,128)(2,1)}, u32[]{:S(2)}) copy-start(bf16[128,1024]{1,0:T(8,128)(2,1)} %copy-done.3) | copy-start | bytes 786436
  223.9 3.8 %copy-start.6 = (bf16[128,1024]{1,0:T(8,128)(2,1)S(1)}, bf16[128,1024]{1,0:T(8,128)(2,1)}, u32[]{:S(2)}) copy-start(bf16[128,1024]{1,0:T(8,128)(2,1)} %copy-done.5) | copy-start | bytes 786436
  226.3 10.1 %collective-permute-start.5 = (bf16[8,16,1024]{2,1,0:T(8,128)(2,1)S(1)}, bf16[8,16,1024]{2,1,0:T(8,128)(2,1)S(1)}, u32[]{:S(2)}, u32[]{:S(2)}) collective-permute-start(bf16[8,16,1024]{2,1,0:T(8,128)(2,1)S(1)} %bitcast.70), channel_id=1, source_target_pairs={{0,16},{1,17},{2,18},{3,19},{4,20},{5,21},{6,22},{7,23},{8,24},{9,... | collective-permute-start | bytes 786440 | tf_op jit(solution)/shard_map/ppermute | solution.py:437
  227.9 0.9 copy-start.10
  227.9 1.0 copy-start.12
  227.9 1.0 copy-start.14
where the time goes:
time: 238 us; the launch traced here: 237 us
  Pallas kernels  163 us (68%)
  waiting for transfers between devices  26.4 us (11%)
  starting transfers between devices  14.9 us (6%)
  local copies, waits for them, and re-layouts  14.7 us (6%)
  other arithmetic  9.53 us (4%)
  matrix products  7.45 us (3%)
    pallas_call x4, Pallas kernels, tick_call(): pl.pallas_call(functools.partial(tick_body, cfg, names, out_names), out_s...  142 us
    pallas_call x2, Pallas kernels, exchange(): pl.pallas_call(functools.partial(exchange_body, len(arrays), n_expert_axi...  20.8 us
    ppermute x2, waiting for transfers between devices, local(): lax.ppermute(state['g_out'], 'section', [(s, s - 1) for s in range(1, n_s...  13.4 us
    ppermute x2, waiting for transfers between devices, local(): lax.ppermute(state['h_next'], 'section', [(s, s + 1) for s in range(last)])  10.1 us
    ppermute x2, starting transfers between devices, local(): lax.ppermute(state['h_next'], 'section', [(s, s + 1) for s in range(last)])  7.75 us
    dot_general x2, matrix products, dot(): lax.dot_general(a, b, ((dims[:1], dims[1:]), ((), ())), precision=precisi...  7.45 us
    unnamed x38, local copies, waits for them, and re-layouts  5.99 us
  transfers between devices with their start and end apart: 6, of which 5 were waited for; matrix products, arithmetic and copies ran while one was open for 5% of the time, Pallas kernels for 0%

commit v1 on v0

v1 whole, which is shorter than its diff:
```python
import functools
import types

import jax
import jax.numpy as jnp
from jax import lax
from jax.experimental import pallas as pl
from jax.experimental.pallas import tpu as pltpu
from jax.sharding import PartitionSpec as P

EPS = 1e-05
CHUNKS = 8
LANES = 128
WEIGHT_STEPS = 4
LAG_F, LAG_T, LAG_B = (1, 2), (1, 2), (2, 4)
F32 = jnp.float32
BF16 = jnp.bfloat16
HIGH = lax.Precision.HIGHEST
ENDS, SEED, HX, GX, ROWS, GATE, BACK, TOP, DU, DOT, FIN = range(11)
KINDS = 11


def dot(a, b, dims, precision=None):
    return lax.dot_general(
        a, b, ((dims[:1], dims[1:]), ((), ())), precision=precision, preferred_element_type=F32
    )


def relay_body(cfg, names, *refs):
    r = types.SimpleNamespace(**dict(zip(names, refs)))
    chunks, n_rank, n_dp, n_sec, tok, cap = cfg
    _, tokens, piece = r.x.shape
    blk, width = r.u_land.shape[2:]
    cells = n_rank * blk
    hidden_width = r.w_dn.shape[0]
    n_expert = n_rank
    last = n_sec - 1
    section = lax.axis_index("section")
    me = lax.axis_index("expert") * n_dp + lax.axis_index("dp")
    send_sem, recv_sem = r.send_sem, r.recv_sem

    def place(step):
        rank = lax.rem(me + step, n_rank)
        return rank, {"expert": lax.div(rank, n_dp), "dp": lax.rem(rank, n_dp)}

    load_gu = pltpu.make_async_copy(r.w_gu, r.gu_buf, r.load_sem.at[0])
    load_dn = pltpu.make_async_copy(r.w_dn, r.dn_buf, r.load_sem.at[1])
    load_gu.start()
    load_dn.start()
    barrier = pltpu.get_barrier_semaphore()
    for step in range(1, n_sec):
        pl.semaphore_signal(
            barrier, inc=1, device_id={"section": lax.rem(section + step, n_sec)},
            device_id_type=pl.DeviceIdType.MESH,
        )
    for step in range(1, n_rank):
        pl.semaphore_signal(
            barrier, inc=1, device_id=place(step)[1], device_id_type=pl.DeviceIdType.MESH
        )
    r.rt[:n_expert] = r.router_t[...]
    r.rt[n_expert:] = r.router_t[...]
    r.acc[...] = jnp.zeros(r.acc.shape, F32)
    r.gain_acc[...] = jnp.zeros(r.gain_acc.shape, F32)

    def iota(shape, axis):
        return lax.broadcasted_iota(jnp.int32, shape, axis)

    def loop(count, body):
        def run(t, carry):
            body(t)
            return carry

        lax.fori_loop(0, count, run, 0)

    def tabulate(c):
        route = r.route[c].astype(F32)
        rows, cols = iota((tokens, tokens), 0), iota((tokens, tokens), 1)
        eye = (rows == cols).astype(F32)
        early = ((lax.div(rows, tok) == lax.div(cols, tok)) & (cols < rows)).astype(F32)
        across = [route[k : k + 1, :] for k in range(2)]
        e = [jnp.sum(eye * v, axis=1, keepdims=True) for v in across]
        within = (lax.div(iota((tokens, 1), 0), tok) * cap).astype(F32)
        inner, cell = [], []
        for k in range(2):
            named = (across[0] == e[k]).astype(F32) + (across[1] == e[k]).astype(F32)
            inner.append(within + jnp.sum(early * named, axis=1, keepdims=True))
            cell.append(e[k] * blk + inner[k])
            r.wide[c, k : k + 1] = across[k]
            r.wide[c, 2 + k : 3 + k] = jnp.sum(eye * cell[k], axis=0, keepdims=True)
        at = iota((tokens, LANES), 1)
        tall = jnp.zeros((tokens, LANES), F32)
        for k, v in enumerate(e + inner + cell):
            tall = jnp.where(at == k, v, tall)
        r.tall[c] = tall

    loop(chunks, tabulate)
    pl.semaphore_wait(barrier, n_rank - 1 + n_sec - 1)

    def push(src, dst, kind, c, device):
        pltpu.make_async_remote_copy(
            src_ref=src, dst_ref=dst, send_sem=send_sem.at[kind, c], recv_sem=recv_sem.at[kind, c],
            device_id=device, device_id_type=pl.DeviceIdType.MESH,
        ).start()

    def spread(src, dst, kind, c):
        for step in range(1, n_rank):
            rank, device = place(step)
            push(src.at[rank], dst.at[me], kind, c, device)
        dst[me] = src[me]

    def settle(ref, sem):
        pltpu.make_async_copy(ref, ref, sem).wait()

    def landed(dst, kind, c):
        settle(dst.at[pl.ds(0, n_rank - 1)], recv_sem.at[kind, c])

    def sent(src, kind, c):
        settle(src.at[pl.ds(0, n_rank - 1)], send_sem.at[kind, c])

    def lanes_of(value):
        return value.reshape(n_rank, 1, LANES)

    lane_of_cell = lax.rem(iota((cells, LANES), 0), blk) == iota((cells, LANES), 1)
    lane_of_cell = lane_of_cell.astype(F32)

    def columns(c):
        tall = r.tall[c]
        e, inner, cell = ([tall[:, 2 * i + k : 2 * i + k + 1] for k in range(2)] for i in range(3))
        return e, inner, cell

    def to_cells(c):
        at = iota((cells, tokens), 0).astype(F32)
        return [(r.wide[c, 2 + k : 3 + k] == at).astype(F32) for k in range(2)]

    def from_cells(cell):
        at = iota((tokens, cells), 1).astype(F32)
        return [(cell[k] == at).astype(F32) for k in range(2)]

    def hits(e):
        at = iota((tokens, n_expert), 1).astype(F32)
        return [(e[k] == at).astype(F32) for k in range(2)]

    def slots(inner):
        at = iota((tokens, LANES), 1).astype(F32)
        return [(inner[k] == at).astype(F32) for k in range(2)]

    def dispatch(place_at, value, out, land, kind, c):
        rows = dot(place_at.astype(BF16), value, (1, 0)).astype(BF16)
        out[...] = rows.reshape(n_rank, blk, width)
        spread(out, land, kind, c)

    def signed(e, l):
        l_high = l.astype(BF16).astype(F32)
        at = iota((tokens, 2 * n_expert), 1)
        which = lax.rem(at, n_expert).astype(F32)
        signs = (e[0] == which).astype(F32) - (e[1] == which).astype(F32)
        return (jnp.where(at < n_expert, l_high, l - l_high) * signs).astype(BF16)

    def add_router(c, cols):
        term = dot(cols, r.u[c], (0, 0))
        r.acc[...] += term[:n_expert] + term[n_expert:]

    def send_tokens(c):
        @pl.when(section == 0)
        def _():
            settle(r.ends.at[c, pl.ds(0, n_sec - 1)], recv_sem.at[ENDS, c])
            r.h[c] = jnp.concatenate(
                [r.x[c]] + [r.ends[c, s] for s in range(1, n_sec)], axis=1
            )

        @pl.when(section > 0)
        def _():
            settle(r.h.at[c], recv_sem.at[HX, c])

        place_at = to_cells(c)
        h = r.h[c].astype(F32)
        inv = lax.rsqrt(jnp.mean(h * h, axis=-1, keepdims=True) + EPS)
        u = (h * inv * r.gain[...]).astype(BF16)
        dispatch(place_at[0] + place_at[1], u, r.u_out.at[c], r.u_land.at[c], ROWS, c)
        r.u[c] = u
        e, inner, _ = columns(c)
        hit = hits(e)
        diff = jnp.sum((hit[0] - hit[1]) * dot(u, r.router_t[...], (1, 1)), axis=1, keepdims=True)
        gate = [jax.nn.sigmoid(diff), jax.nn.sigmoid(-diff)]
        at = iota((tokens, LANES), 1)
        r.keep[c] = jnp.where(at == 0, gate[0], jnp.where(at == 1, gate[1], inv))

        @pl.when(section == last)
        def _():
            slot = slots(inner)
            at = iota((n_expert, tokens), 0).astype(F32)
            packed = sum(
                dot((r.wide[c, k : k + 1] == at).astype(F32), gate[k] * slot[k], (1, 0), HIGH)
                for k in range(2)
            )
            r.gate_out[c] = lanes_of(packed)
            spread(r.gate_out.at[c], r.gate_land.at[c], GATE, c)

    def expert_up(c):
        @pl.when(c == 0)
        def _():
            load_gu.wait()
            load_dn.wait()

        landed(r.u_land.at[c], ROWS, c)
        rows = r.u_land[c].reshape(cells, width)
        r.rows[c] = rows
        gate_up = dot(rows, r.gu_buf[...], (1, 0))
        a, b = gate_up[:, :hidden_width], gate_up[:, hidden_width:]
        sig = jax.nn.sigmoid(a)
        silu = a * sig
        hidden = (silu * b).astype(BF16)
        r.hidden[c] = hidden
        r.slope[c, :, :hidden_width] = b * (sig * (1.0 + a * (1.0 - sig)))
        r.slope[c, :, hidden_width:] = silu
        return hidden

    def expert_forward(c):
        hidden = expert_up(c)
        y = dot(hidden, r.dn_buf[...], (1, 0)).astype(BF16)
        r.y_out[c] = y.reshape(n_rank, blk, width)
        spread(r.y_out.at[c], r.y_land.at[c], BACK, c)

    def expert_down(c, d_hidden):
        slope = r.slope[c]
        q = jnp.concatenate(
            [d_hidden * slope[:, :hidden_width], d_hidden * slope[:, hidden_width:]], axis=1
        ).astype(BF16)
        r.q[c] = q
        du = dot(q, r.gu_buf[...], (1, 1)).astype(BF16)
        r.du_out[c] = du.reshape(n_rank, blk, width)
        spread(r.du_out.at[c], r.du_land.at[c], DU, c)

    def expert_backward(c):
        landed(r.g_land.at[c], TOP, c)
        top = r.g_land[c].reshape(cells, width)
        r.dy[c] = top
        expert_down(c, dot(top, r.dn_buf[...], (1, 1)))

    def expert_last(c):
        hidden = expert_up(c)
        landed(r.g_land.at[c], TOP, c)
        landed(r.gate_land.at[c], GATE, c)
        spread_rows = (lax.div(iota((cells, n_rank), 0), blk) == iota((cells, n_rank), 1)).astype(F32)
        wide = dot(spread_rows, r.gate_land[c].reshape(n_rank, LANES), (1, 0), HIGH)
        gate = jnp.sum(wide * lane_of_cell, axis=1, keepdims=True)
        top = r.g_land[c].reshape(cells, width)
        plain = dot(top, r.dn_buf[...], (1, 1))
        expert_down(c, plain * gate)
        share = jnp.sum(plain * hidden.astype(F32), axis=1, keepdims=True)
        gather = (iota((n_rank, cells), 0) == lax.div(iota((n_rank, cells), 1), blk)).astype(F32)
        r.dot_out[c] = lanes_of(dot(gather, share * lane_of_cell, (1, 0), HIGH))
        spread(r.dot_out.at[c], r.dot_land.at[c], DOT, c)
        r.dy[c] = (top.astype(F32) * gate).astype(BF16)

    def combine_forward(c):
        pick = from_cells(columns(c)[2])
        keep = r.keep[c]
        landed(r.y_land.at[c], BACK, c)
        back = r.y_land[c].reshape(cells, width)
        picked = dot(jnp.concatenate(pick, axis=0).astype(BF16), back, (1, 0))
        h = r.h[c].astype(F32)
        up = h + keep[:, 0:1] * picked[:tokens] + keep[:, 1:2] * picked[tokens:]
        r.h_out[c] = up.astype(BF16)
        push(r.h_out.at[c], r.h.at[c], HX, c, {"section": section + 1})
        r.lean[c] = picked[:tokens] - picked[tokens:]

    def send_seed(c):
        settle(r.ends.at[c, pl.ds(0, n_sec - 1)], recv_sem.at[SEED, c])
        top = jnp.concatenate([r.ends[c, s] for s in range(last)] + [r.cot[c]], axis=1)
        r.g[c] = top
        place_at = to_cells(c)
        dispatch(place_at[0] + place_at[1], top, r.g_out.at[c], r.g_land.at[c], TOP, c)

    def send_top(c):
        place_at = jnp.concatenate(to_cells(c), axis=1)
        keep = r.keep[c]
        settle(r.g.at[c], recv_sem.at[GX, c])
        top = r.g[c].astype(F32)
        scaled = [(keep[:, k : k + 1] * top).astype(BF16) for k in range(2)]
        dispatch(
            place_at, jnp.concatenate(scaled, axis=0), r.g_out.at[c], r.g_land.at[c], TOP, c
        )
        share = jnp.sum(top * r.lean[c], axis=1, keepdims=True)
        cols = signed(columns(c)[0], keep[:, 0:1] * keep[:, 1:2] * share)
        r.cols[c] = cols
        add_router(c, cols)

        @pl.when(c == chunks - 1)
        def _():
            router_start()

    def finish_last(c):
        e, inner, cell = columns(c)
        hit, slot = hits(e), slots(inner)
        keep = r.keep[c]
        landed(r.dot_land.at[c], DOT, c)
        shares = r.dot_land[c].reshape(n_rank, LANES)
        wide = [dot(hit[k], shares, (1, 0), HIGH) * slot[k] for k in range(2)]
        share = jnp.sum(wide[0] - wide[1], axis=1, keepdims=True)
        cols = signed(e, keep[:, 0:1] * keep[:, 1:2] * share)
        finish(c, cols)
        add_router(c, cols)

    def finish(c, cols):
        pick = from_cells(columns(c)[2])
        inv = r.keep[c][:, 2:3]
        extra = dot(cols, r.rt[...], (1, 0))
        hn = r.h[c].astype(F32) * inv
        landed(r.du_land.at[c], DU, c)
        back = r.du_land[c].reshape(cells, width)
        du = dot((pick[0] + pick[1]).astype(BF16), back, (1, 0)) + extra
        scaled = du * r.gain[...]
        projection = jnp.mean(scaled * hn, axis=-1, keepdims=True)
        low = (r.g[c].astype(F32) + inv * (scaled - hn * projection)).astype(BF16)
        r.low[c] = low

        @pl.when(section > 0)
        def _():
            push(r.low.at[c], r.g.at[c], GX, c, {"section": section - 1})

        @pl.when(section == 0)
        def _():
            r.gin[c] = low[:, :piece]
            for s in range(1, n_sec):
                r.fin[c, s - 1] = low[:, s * piece : (s + 1) * piece]
                push(r.fin.at[c, s - 1], r.gin.at[c], FIN, c, {"section": s})

        r.gain_acc[...] += jnp.sum(du * hn, axis=0, keepdims=True)

    part = width // n_rank

    def share_out(src, dst, which):
        for step in range(1, n_rank):
            rank, device = place(step)
            pltpu.make_async_remote_copy(
                src_ref=src(rank), dst_ref=dst.at[me],
                send_sem=r.sum_sem.at[2 * which], recv_sem=r.sum_sem.at[2 * which + 1],
                device_id=device, device_id_type=pl.DeviceIdType.MESH,
            ).start()
        dst[me] = src(me)[...]

    def shared(dst, which, side):
        settle(dst.at[pl.ds(0, n_rank - 1)], r.sum_sem.at[2 * which + side])

    def router_start():
        for rank in range(n_rank):
            r.part_out[rank] = r.acc[:, rank * part : (rank + 1) * part].astype(BF16)
        share_out(lambda rank: r.part_out.at[rank], r.part_land, 0)

    def router_middle():
        shared(r.part_land, 0, 1)
        r.tot_out[...] = jnp.sum(r.part_land[...].astype(F32), axis=0).astype(BF16)
        share_out(lambda rank: r.tot_out, r.tot_land, 1)

    for c in range(chunks):
        @pl.when(section > 0)
        def _():
            push(r.x.at[c], r.ends.at[c, section], ENDS, c, {"section": 0})

        @pl.when(section < last)
        def _():
            push(r.cot.at[c], r.ends.at[c, section], SEED, c, {"section": last})

    def guarded(t, body):
        @pl.when((t >= 0) & (t < chunks))
        def _():
            body(jnp.clip(t, 0, chunks - 1))

    def rounds(stages):
        def step(t):
            for lag, body in stages:
                guarded(t - lag, body)

        loop(chunks + max(lag for lag, _ in stages), step)

    @pl.when(section == last)
    def _():
        loop(chunks, send_seed)
        rounds(((0, send_tokens), (LAG_T[0], expert_last), (LAG_T[1], finish_last)))
        router_start()
        router_middle()

    @pl.when(section < last)
    def _():
        rounds(((0, send_tokens), (LAG_F[0], expert_forward), (LAG_F[1], combine_forward)))

        def middle(c):
            @pl.when(c == chunks - 1)
            def _():
                router_middle()

        rounds((
            (0, send_top), (LAG_B[0], expert_backward), (LAG_B[0], middle),
            (LAG_B[1], lambda c: finish(c, r.cols[c])),
        ))

    lines = width // LANES
    r.gain_out[...] = jnp.concatenate(
        [r.gain_acc[:, i * LANES : (i + 1) * LANES] for i in range(lines)], axis=0
    ).astype(BF16)
    share_out(lambda rank: r.gain_out, r.gain_land, 2)
    shared(r.tot_land, 1, 1)
    for rank in range(n_rank):
        r.grad_router[:, rank * part : (rank + 1) * part] = r.tot_land[rank].astype(F32)
    shared(r.gain_land, 2, 1)
    total = jnp.sum(r.gain_land[...].astype(F32), axis=0)
    for i in range(lines):
        r.grad_gain[:, i * LANES : (i + 1) * LANES] = total[i : i + 1]
    shared(r.part_land, 0, 0)
    shared(r.tot_land, 1, 0)
    shared(r.gain_land, 2, 0)

    for c in range(chunks):
        for kind, ref in ((ROWS, r.u_out), (TOP, r.g_out), (DU, r.du_out)):
            sent(ref.at[c], kind, c)

        @pl.when(section == last)
        def _():
            sent(r.gate_out.at[c], GATE, c)
            sent(r.dot_out.at[c], DOT, c)

        @pl.when(section < last)
        def _():
            sent(r.y_out.at[c], BACK, c)
            settle(r.h_out.at[c], send_sem.at[HX, c])
            settle(r.cot.at[c], send_sem.at[SEED, c])

        @pl.when(section == 0)
        def _():
            settle(r.fin.at[c], send_sem.at[FIN, c])

        @pl.when(section > 0)
        def _():
            settle(r.x.at[c], send_sem.at[ENDS, c])
            settle(r.low.at[c], send_sem.at[GX, c])
            settle(r.gin.at[c], recv_sem.at[FIN, c])


def weight_body(rows, q, hidden, dy, *refs):
    grad_gu, grad_dn = refs[len(refs) // 2 - 1 : len(refs) // 2 + 1]
    grad_gu[...] = dot(rows[...], q[...], (0, 0))
    grad_dn[...] = dot(hidden[...], dy[...], (0, 0))

    @pl.when(pl.program_id(0) == 0)
    def _():
        count = (len(refs) - 2) // 2
        for given, kept in zip(refs[:count], refs[count + 2 :]):
            kept[...] = given[...]


def weight_grads(rows, q, hidden, dy, *others):
    count, width = rows.shape
    hidden_width = hidden.shape[1]
    steps = WEIGHT_STEPS

    def whole(a):
        return pl.BlockSpec(a.shape, lambda i: (0,) * a.ndim)

    return pl.pallas_call(
        weight_body,
        grid=(steps,),
        out_shape=[
            jax.ShapeDtypeStruct((width, 2 * hidden_width), F32),
            jax.ShapeDtypeStruct((hidden_width, width), F32),
        ]
        + [jax.ShapeDtypeStruct(a.shape, a.dtype) for a in others],
        in_specs=[
            pl.BlockSpec((count, width // steps), lambda i: (0, i)),
            pl.BlockSpec((count, 2 * hidden_width), lambda i: (0, 0)),
            pl.BlockSpec((count, hidden_width // steps), lambda i: (0, i)),
            pl.BlockSpec((count, width), lambda i: (0, 0)),
        ]
        + [whole(a) for a in others],
        out_specs=[
            pl.BlockSpec((width // steps, 2 * hidden_width), lambda i: (i, 0)),
            pl.BlockSpec((hidden_width // steps, width), lambda i: (i, 0)),
        ]
        + [whole(a) for a in others],
        compiler_params=pltpu.CompilerParams(vmem_limit_bytes=60 * 1024 * 1024),
    )(rows, q, hidden, dy, *others)


def local(x_in, cotangent, route_ids, norm_gain, router, w_gate_up, w_down):
    micro, tok, piece = x_in.shape
    n_sec = lax.axis_size("section")
    n_dp = lax.axis_size("dp")
    n_rank = lax.axis_size("expert") * n_dp
    per_rank, hidden_width, width = w_down.shape[1:]
    assert per_rank == 1 and n_sec > 1
    cap = tok * 2 * 9 // (8 * n_rank)
    chunks = CHUNKS if micro % CHUNKS == 0 else 1
    per = micro // chunks
    tokens, blk = per * tok, per * cap
    cells = n_rank * blk
    part = width // n_rank
    args = dict(
        x=x_in.reshape(chunks, tokens, piece), cot=cotangent.reshape(chunks, tokens, piece),
        route=jnp.transpose(route_ids.reshape(chunks, tokens, 2), (0, 2, 1)),
        gain=norm_gain, router_t=router[0].T,
        w_gu=w_gate_up[0, 0], w_dn=w_down[0, 0],
    )
    outs = dict(
        rows=((chunks, cells, width), BF16), q=((chunks, cells, 2 * hidden_width), BF16),
        hidden=((chunks, cells, hidden_width), BF16), dy=((chunks, cells, width), BF16),
        gin=((chunks, tokens, piece), BF16), grad_router=((n_rank, width), F32),
        grad_gain=((1, width), F32),
    )
    exchanged = ((chunks, n_rank, blk, width), BF16)
    token_rows = ((chunks, tokens, width), BF16)
    line = ((chunks, n_rank, 1, LANES), F32)
    scratch = dict(
        gu_buf=(w_gate_up[0, 0].shape, BF16), dn_buf=(w_down[0, 0].shape, BF16),
        rt=((2 * n_rank, width), BF16), acc=((n_rank, width), F32), gain_acc=((1, width), F32),
        tall=((chunks, tokens, LANES), F32), wide=((chunks, 8, tokens), F32),
        lean=((chunks, tokens, width), F32), cols=((chunks, tokens, 2 * n_rank), BF16),
        gain_out=((width // LANES, LANES), BF16), gain_land=((n_rank, width // LANES, LANES), BF16),
        ends=((chunks, n_sec, tokens, piece), BF16), fin=((chunks, n_sec - 1, tokens, piece), BF16),
        h=token_rows, u=token_rows, g=token_rows, h_out=token_rows, low=token_rows,
        keep=((chunks, tokens, LANES), F32), slope=((chunks, cells, 2 * hidden_width), F32),
        part_out=((n_rank, n_rank, part), BF16), part_land=((n_rank, n_rank, part), BF16),
        tot_out=((n_rank, part), BF16), tot_land=((n_rank, n_rank, part), BF16),
        u_out=exchanged, u_land=exchanged, y_out=exchanged, y_land=exchanged,
        g_out=exchanged, g_land=exchanged, du_out=exchanged, du_land=exchanged,
        gate_out=line, gate_land=line, dot_out=line, dot_land=line,
    )
    sems = dict(load_sem=(2,), send_sem=(KINDS, chunks), recv_sem=(KINDS, chunks), sum_sem=(6,))
    vmem = pl.BlockSpec(memory_space=pltpu.VMEM)
    hbm = pl.BlockSpec(memory_space=pl.ANY)
    cfg = (chunks, n_rank, n_dp, n_sec, tok, cap)
    made = pl.pallas_call(
        functools.partial(relay_body, cfg, list(args) + list(outs) + list(scratch) + list(sems)),
        out_shape=[jax.ShapeDtypeStruct(*v) for v in outs.values()],
        in_specs=[hbm if k in ("w_gu", "w_dn") else vmem for k in args],
        out_specs=[vmem] * len(outs),
        scratch_shapes=[pltpu.VMEM(*v) for v in scratch.values()]
        + [pltpu.SemaphoreType.DMA(v) for v in sems.values()],
        compiler_params=pltpu.CompilerParams(
            collective_id=1, has_side_effects=True, vmem_limit_bytes=56 * 1024 * 1024
        ),
    )(*args.values())
    made = types.SimpleNamespace(**dict(zip(outs, made)))

    def flat(value):
        return value.reshape(chunks * cells, -1)

    grad_gu, grad_dn, gin, grad_router, grad_gain = weight_grads(
        flat(made.rows), flat(made.q), flat(made.hidden), flat(made.dy),
        made.gin, made.grad_router, made.grad_gain,
    )
    return (
        gin.reshape(micro, tok, piece), grad_gu[None, None], grad_dn[None, None],
        grad_router.T[None], grad_gain,
    )


def solution(mesh):
    in_specs = (
        P(None, ("expert", "dp"), "section"),
        P(None, ("expert", "dp"), "section"),
        P("section", None, ("expert", "dp"), None),
        P("section", None),
        P("section", None, None),
        P("section", ("expert", "dp"), None, None),
        P("section", ("expert", "dp"), None, None),
    )
    out_specs = (
        P(None, ("expert", "dp"), "section"),
        P("section", ("expert", "dp"), None, None),
        P("section", ("expert", "dp"), None, None),
        P("section", None, None),
        P("section", None),
    )
    return jax.shard_map(local, mesh=mesh, in_specs=in_specs, out_specs=out_specs, check_vma=False)
```

time: 238 us -> 127 us (0.53)
  Pallas kernels: 163 us -> 127 us
  waiting for transfers between devices: 26.4 us -> 0 us
  starting transfers between devices: 14.9 us -> 0 us
  local copies, waits for them, and re-layouts: 14.7 us -> 0 us
  other arithmetic: 9.53 us -> 0 us
  matrix products: 7.45 us -> 0 us
    pallas_call x6 -> x2, Pallas kernels: 163 us -> 127 us  [the longest x1 119 us: local(): pl.pallas_call(functools.partial(relay_body, cfg, list(args) + list(outs)...]
    ppermute x6 -> x0, waiting for transfers between devices: 26.4 us -> none  [the longest x2 13.4 us: local(): lax.ppermute(state['g_out'], 'section', [(s, s - 1) for s in range(1, n_s...]
    ppermute x6 -> x0, starting transfers between devices: 14.9 us -> none  [the longest x2 7.75 us: local(): lax.ppermute(state['h_next'], 'section', [(s, s + 1) for s in range(last)])]
    dot_general x2 -> x0, matrix products: 7.45 us -> none  [dot(): lax.dot_general(a, b, ((dims[:1], dims[1:]), ((), ())), precision=precisi...]
    unnamed x38 -> x0, local copies, waits for them, and re-layouts: 5.99 us -> none
    slice x4 -> x0, local copies, waits for them, and re-layouts: 3.78 us -> none  [the longest x1 2.26 us: local(): grad_in = out[:, :, 0]]
    reduce_sum x4 -> x0, other arithmetic: 3.18 us -> none  [the longest x1 1.14 us: place_cells(): slot = jnp.sum(hits * before[:, :, None, :], axis=3)]
    select_n x5 -> x0, other arithmetic: 2.97 us -> none  [the longest x1 1.84 us: ends_gather(): jnp.where(section == source, x_in, cotangent)]
  transfers between devices with their start and end apart: 6 -> 0, of which waited for: 5 -> 0; matrix products, arithmetic and copies ran while one was open for 5% -> 0% of each run, Pallas kernels for 0% -> 0%
where the time goes in v1:
time: 127 us
  Pallas kernels  127 us (100%)
    pallas_call x1, Pallas kernels, local(): pl.pallas_call(functools.partial(relay_body, cfg, list(args) + list(outs)...  119 us
    pallas_call x1, Pallas kernels, weight_grads(): pl.pallas_call(weight_body, grid=(steps,), out_shape=[jax.ShapeDtypeStruc...  7.37 us

profile of v1, /device:TPU:0, one launch (start us, length us, event | category | flops | bytes accessed | tf_op | source)
XLA Modules:
  0.0 127.2 jit_solution(423532074735690474)
XLA Ops:
  0.6 119.1 %shard_map.110 = (bf16[8,32,2048]{2,1,0:T(8,128)(2,1)}, bf16[8,32,1024]{2,1,0:T(8,128)(2,1)}, bf16[8,32,512]{2,1,0:T(8,128)(2,1)}, bf16[8,32,2048]{2,1,0:T(8,128...) custom-call(bf16[8,16,1024]{2,1,0:T(8,128)(2,1)} %refs_0_.1, ...), custom_call_target="tpu_custom_call" | custom-call | tf_op jit(solution)/shard_map/pallas_call | solution.py:531
  119.8 7.4 %shard_map.111 = (f32[2048,1024]{1,0:T(8,128)}, f32[512,2048]{1,0:T(8,128)}, bf16[8,16,1024]{2,1,0:T(8,128)(2,1)}, f32[16,2048]{1,0:T(8,128)}, f32[1,2048]{1,0:T(1,128)}) custom-call(bf16[256,2048]{1,0:T(8,128)(2,1)} %bitcast.19, bf16[256,1024]{1,0:T(8,128)(2,1)} %bitcast.21, bf16[256,512]{1,0:T(8,128)(2,1)} %bitcast.22, bf16[256,2048]{1,0:T(8,128)(2,1)} %bitcast.20, ...), custom_call_target="tpu_custom_call" | custom-call | tf_op jit(solution)/shard_map/pallas_call | solution.py:460

commit v2 on v1

--- a/solution.py
+++ b/solution.py
@@ -12,7 +12,10 @@
 CHUNKS = 8
 LANES = 128
 WEIGHT_STEPS = 4
-LAG_F, LAG_T, LAG_B = (1, 2), (1, 2), (2, 4)
+LIMIT_RELAY = 56
+LIMIT_WEIGHT = 48
+LAG_S = 5
+LAG_F, LAG_T, LAG_B = (2, 3), (1, 2), (2, 4)
 F32 = jnp.float32
 BF16 = jnp.bfloat16
 HIGH = lax.Precision.HIGHEST
@@ -45,6 +48,15 @@
 
     load_gu = pltpu.make_async_copy(r.w_gu, r.gu_buf, r.load_sem.at[0])
     load_dn = pltpu.make_async_copy(r.w_dn, r.dn_buf, r.load_sem.at[1])
+    loads = [
+        pltpu.make_async_copy(src, dst, r.load_sem.at[2 + i])
+        for i, (src, dst) in enumerate((
+            (r.x_hbm, r.x), (r.cot_hbm, r.cot), (r.route_hbm, r.route), (r.gain_hbm, r.gain),
+            (r.router_hbm, r.router_t),
+        ))
+    ]
+    for load in loads:
+        load.start()
     load_gu.start()
     load_dn.start()
     barrier = pltpu.get_barrier_semaphore()
@@ -57,11 +69,6 @@
         pl.semaphore_signal(
             barrier, inc=1, device_id=place(step)[1], device_id_type=pl.DeviceIdType.MESH
         )
-    r.rt[:n_expert] = r.router_t[...]
-    r.rt[n_expert:] = r.router_t[...]
-    r.acc[...] = jnp.zeros(r.acc.shape, F32)
-    r.gain_acc[...] = jnp.zeros(r.gain_acc.shape, F32)
-
     def iota(shape, axis):
         return lax.broadcasted_iota(jnp.int32, shape, axis)
 
@@ -93,14 +100,32 @@
             tall = jnp.where(at == k, v, tall)
         r.tall[c] = tall
 
-    loop(chunks, tabulate)
     pl.semaphore_wait(barrier, n_rank - 1 + n_sec - 1)
+    for load in loads:
+        load.wait()
 
     def push(src, dst, kind, c, device):
         pltpu.make_async_remote_copy(
             src_ref=src, dst_ref=dst, send_sem=send_sem.at[kind, c], recv_sem=recv_sem.at[kind, c],
             device_id=device, device_id_type=pl.DeviceIdType.MESH,
         ).start()
+
+    for c in range(chunks):
+        @pl.when(section > 0)
+        def _():
+            push(r.x.at[c], r.ends.at[c, section], ENDS, c, {"section": 0})
+
+        @pl.when(section < last)
+        def _():
+            push(r.cot.at[c], r.ends.at[c, section], SEED, c, {"section": last})
+
+    r.rt[:n_expert] = r.router_t[...]
+    r.rt[n_expert:] = r.router_t[...]
+    r.acc[...] = jnp.zeros(r.acc.shape, F32)
+    r.gain_acc[...] = jnp.zeros(r.gain_acc.shape, F32)
+
+    for c in range(chunks):
+        tabulate(c)
 
     def spread(src, dst, kind, c):
         for step in range(1, n_rank):
@@ -200,7 +225,6 @@
         @pl.when(c == 0)
         def _():
             load_gu.wait()
-            load_dn.wait()
 
         landed(r.u_land.at[c], ROWS, c)
         rows = r.u_land[c].reshape(cells, width)
@@ -217,6 +241,11 @@
 
     def expert_forward(c):
         hidden = expert_up(c)
+
+        @pl.when(c == 0)
+        def _():
+            load_dn.wait()
+
         y = dot(hidden, r.dn_buf[...], (1, 0)).astype(BF16)
         r.y_out[c] = y.reshape(n_rank, blk, width)
         spread(r.y_out.at[c], r.y_land.at[c], BACK, c)
@@ -230,6 +259,15 @@
         du = dot(q, r.gu_buf[...], (1, 1)).astype(BF16)
         r.du_out[c] = du.reshape(n_rank, blk, width)
         spread(r.du_out.at[c], r.du_land.at[c], DU, c)
+        both = r.rows[c].astype(F32) * du.astype(F32)
+        r.gain_acc[...] += jnp.sum(both, axis=0, keepdims=True)
+
+        @pl.when(c == chunks - 1)
+        def _():
+            r.gain_out[...] = jnp.concatenate(
+                [r.gain_acc[:, i * LANES : (i + 1) * LANES] for i in range(lines)], axis=0
+            ).astype(BF16)
+            share_out(lambda rank: r.gain_out, r.gain_land, 2)
 
     def expert_backward(c):
         landed(r.g_land.at[c], TOP, c)
@@ -239,13 +277,12 @@
 
     def expert_last(c):
         hidden = expert_up(c)
-        landed(r.g_land.at[c], TOP, c)
         landed(r.gate_land.at[c], GATE, c)
         spread_rows = (lax.div(iota((cells, n_rank), 0), blk) == iota((cells, n_rank), 1)).astype(F32)
         wide = dot(spread_rows, r.gate_land[c].reshape(n_rank, LANES), (1, 0), HIGH)
         gate = jnp.sum(wide * lane_of_cell, axis=1, keepdims=True)
         top = r.g_land[c].reshape(cells, width)
-        plain = dot(top, r.dn_buf[...], (1, 1))
+        plain = r.plain[c]
         expert_down(c, plain * gate)
         share = jnp.sum(plain * hidden.astype(F32), axis=1, keepdims=True)
         gather = (iota((n_rank, cells), 0) == lax.div(iota((n_rank, cells), 1), blk)).astype(F32)
@@ -271,6 +308,14 @@
         r.g[c] = top
         place_at = to_cells(c)
         dispatch(place_at[0] + place_at[1], top, r.g_out.at[c], r.g_land.at[c], TOP, c)
+
+    def expert_seed(c):
+        @pl.when(c == 0)
+        def _():
+            load_dn.wait()
+
+        landed(r.g_land.at[c], TOP, c)
+        r.plain[c] = dot(r.g_land[c].reshape(cells, width), r.dn_buf[...], (1, 1))
 
     def send_top(c):
         place_at = jnp.concatenate(to_cells(c), axis=1)
@@ -326,9 +371,7 @@
                 r.fin[c, s - 1] = low[:, s * piece : (s + 1) * piece]
                 push(r.fin.at[c, s - 1], r.gin.at[c], FIN, c, {"section": s})
 
-        r.gain_acc[...] += jnp.sum(du * hn, axis=0, keepdims=True)
-
-    part = width // n_rank
+    part, lines = width // n_rank, width // LANES
 
     def share_out(src, dst, which):
         for step in range(1, n_rank):
@@ -353,15 +396,6 @@
         r.tot_out[...] = jnp.sum(r.part_land[...].astype(F32), axis=0).astype(BF16)
         share_out(lambda rank: r.tot_out, r.tot_land, 1)
 
-    for c in range(chunks):
-        @pl.when(section > 0)
-        def _():
-            push(r.x.at[c], r.ends.at[c, section], ENDS, c, {"section": 0})
-
-        @pl.when(section < last)
-        def _():
-            push(r.cot.at[c], r.ends.at[c, section], SEED, c, {"section": last})
-
     def guarded(t, body):
         @pl.when((t >= 0) & (t < chunks))
         def _():
@@ -376,7 +410,7 @@
 
     @pl.when(section == last)
     def _():
-        loop(chunks, send_seed)
+        rounds(((0, send_seed), (LAG_S, expert_seed)))
         rounds(((0, send_tokens), (LAG_T[0], expert_last), (LAG_T[1], finish_last)))
         router_start()
         router_middle()
@@ -395,18 +429,15 @@
             (LAG_B[1], lambda c: finish(c, r.cols[c])),
         ))
 
-    lines = width // LANES
-    r.gain_out[...] = jnp.concatenate(
-        [r.gain_acc[:, i * LANES : (i + 1) * LANES] for i in range(lines)], axis=0
-    ).astype(BF16)
-    share_out(lambda rank: r.gain_out, r.gain_land, 2)
     shared(r.tot_land, 1, 1)
     for rank in range(n_rank):
         r.grad_router[:, rank * part : (rank + 1) * part] = r.tot_land[rank].astype(F32)
     shared(r.gain_land, 2, 1)
     total = jnp.sum(r.gain_land[...].astype(F32), axis=0)
+    routed = jnp.sum(r.router_t[...].astype(F32) * r.grad_router[...], axis=0, keepdims=True)
     for i in range(lines):
-        r.grad_gain[:, i * LANES : (i + 1) * LANES] = total[i : i + 1]
+        lane = slice(i * LANES, (i + 1) * LANES)
+        r.grad_gain[:, lane] = (total[i : i + 1] + routed[:, lane]) / r.gain[:, lane]
     shared(r.part_land, 0, 0)
     shared(r.tot_land, 1, 0)
     shared(r.gain_land, 2, 0)
@@ -437,47 +468,42 @@
             settle(r.gin.at[c], recv_sem.at[FIN, c])
 
 
-def weight_body(rows, q, hidden, dy, *refs):
-    grad_gu, grad_dn = refs[len(refs) // 2 - 1 : len(refs) // 2 + 1]
-    grad_gu[...] = dot(rows[...], q[...], (0, 0))
-    grad_dn[...] = dot(hidden[...], dy[...], (0, 0))
-
-    @pl.when(pl.program_id(0) == 0)
-    def _():
-        count = (len(refs) - 2) // 2
-        for given, kept in zip(refs[:count], refs[count + 2 :]):
-            kept[...] = given[...]
+def weight_body(steps, n_other, *refs):
+    rows, q, hidden, dy = refs[:4]
+    others = refs[4 : 4 + n_other]
+    grad_gu, grad_dn = refs[4 + n_other : 6 + n_other]
+    kept = refs[6 + n_other : 6 + 2 * n_other]
+    up, down, sem = refs[6 + 2 * n_other :]
+    for given, copy in zip(others, kept):
+        copy[...] = given[...]
+    writes = []
+    for i in range(steps):
+        for k, (buf, out, left, right) in enumerate(
+            ((up, grad_gu, rows, q), (down, grad_dn, hidden, dy))
+        ):
+            size = buf.shape[0] // steps
+            at = pl.ds(i * size, size)
+            buf[at] = dot(left[:, at], right[...], (0, 0))
+            write = pltpu.make_async_copy(buf.at[at], out.at[at], sem.at[k, i])
+            write.start()
+            writes.append(write)
+    for write in writes:
+        write.wait()
 
 
 def weight_grads(rows, q, hidden, dy, *others):
-    count, width = rows.shape
-    hidden_width = hidden.shape[1]
-    steps = WEIGHT_STEPS
-
-    def whole(a):
-        return pl.BlockSpec(a.shape, lambda i: (0,) * a.ndim)
-
+    width, hidden_width = rows.shape[1], hidden.shape[1]
+    shapes = [(width, 2 * hidden_width), (hidden_width, width)]
+    vmem, hbm = pl.BlockSpec(memory_space=pltpu.VMEM), pl.BlockSpec(memory_space=pltpu.HBM)
     return pl.pallas_call(
-        weight_body,
-        grid=(steps,),
-        out_shape=[
-            jax.ShapeDtypeStruct((width, 2 * hidden_width), F32),
-            jax.ShapeDtypeStruct((hidden_width, width), F32),
-        ]
+        functools.partial(weight_body, WEIGHT_STEPS, len(others)),
+        out_shape=[jax.ShapeDtypeStruct(v, F32) for v in shapes]
         + [jax.ShapeDtypeStruct(a.shape, a.dtype) for a in others],
-        in_specs=[
-            pl.BlockSpec((count, width // steps), lambda i: (0, i)),
-            pl.BlockSpec((count, 2 * hidden_width), lambda i: (0, 0)),
-            pl.BlockSpec((count, hidden_width // steps), lambda i: (0, i)),
-            pl.BlockSpec((count, width), lambda i: (0, 0)),
-        ]
-        + [whole(a) for a in others],
-        out_specs=[
-            pl.BlockSpec((width // steps, 2 * hidden_width), lambda i: (i, 0)),
-            pl.BlockSpec((hidden_width // steps, width), lambda i: (i, 0)),
-        ]
-        + [whole(a) for a in others],
-        compiler_params=pltpu.CompilerParams(vmem_limit_bytes=60 * 1024 * 1024),
+        in_specs=[vmem] * (4 + len(others)),
+        out_specs=[hbm] * 2 + [vmem] * len(others),
+        scratch_shapes=[pltpu.VMEM(v, F32) for v in shapes]
+        + [pltpu.SemaphoreType.DMA((2, WEIGHT_STEPS))],
+        compiler_params=pltpu.CompilerParams(vmem_limit_bytes=LIMIT_WEIGHT * 1024 * 1024),
     )(rows, q, hidden, dy, *others)
 
 
@@ -495,9 +521,9 @@
     cells = n_rank * blk
     part = width // n_rank
     args = dict(
-        x=x_in.reshape(chunks, tokens, piece), cot=cotangent.reshape(chunks, tokens, piece),
-        route=jnp.transpose(route_ids.reshape(chunks, tokens, 2), (0, 2, 1)),
-        gain=norm_gain, router_t=router[0].T,
+        x_hbm=x_in.reshape(chunks, tokens, piece), cot_hbm=cotangent.reshape(chunks, tokens, piece),
+        route_hbm=jnp.transpose(route_ids.reshape(chunks, tokens, 2), (0, 2, 1)),
+        gain_hbm=norm_gain, router_hbm=router[0].T,
         w_gu=w_gate_up[0, 0], w_dn=w_down[0, 0],
     )
     outs = dict(
@@ -510,10 +536,13 @@
     token_rows = ((chunks, tokens, width), BF16)
     line = ((chunks, n_rank, 1, LANES), F32)
     scratch = dict(
+        x=((chunks, tokens, piece), BF16), cot=((chunks, tokens, piece), BF16),
+        route=((chunks, 2, tokens), jnp.int32), gain=((1, width), F32),
+        router_t=((n_rank, width), BF16),
         gu_buf=(w_gate_up[0, 0].shape, BF16), dn_buf=(w_down[0, 0].shape, BF16),
         rt=((2 * n_rank, width), BF16), acc=((n_rank, width), F32), gain_acc=((1, width), F32),
         tall=((chunks, tokens, LANES), F32), wide=((chunks, 8, tokens), F32),
-        lean=((chunks, tokens, width), F32), cols=((chunks, tokens, 2 * n_rank), BF16),
+        plain=((chunks, cells, hidden_width), F32), lean=((chunks, tokens, width), F32), cols=((chunks, tokens, 2 * n_rank), BF16),
         gain_out=((width // LANES, LANES), BF16), gain_land=((n_rank, width // LANES, LANES), BF16),
         ends=((chunks, n_sec, tokens, piece), BF16), fin=((chunks, n_sec - 1, tokens, piece), BF16),
         h=token_rows, u=token_rows, g=token_rows, h_out=token_rows, low=token_rows,
@@ -524,19 +553,19 @@
         g_out=exchanged, g_land=exchanged, du_out=exchanged, du_land=exchanged,
         gate_out=line, gate_land=line, dot_out=line, dot_land=line,
     )
-    sems = dict(load_sem=(2,), send_sem=(KINDS, chunks), recv_sem=(KINDS, chunks), sum_sem=(6,))
+    sems = dict(load_sem=(7,), send_sem=(KINDS, chunks), recv_sem=(KINDS, chunks), sum_sem=(6,))
     vmem = pl.BlockSpec(memory_space=pltpu.VMEM)
-    hbm = pl.BlockSpec(memory_space=pl.ANY)
+    hbm = pl.BlockSpec(memory_space=pltpu.HBM)
     cfg = (chunks, n_rank, n_dp, n_sec, tok, cap)
     made = pl.pallas_call(
         functools.partial(relay_body, cfg, list(args) + list(outs) + list(scratch) + list(sems)),
-        out_shape=[jax.ShapeDtypeStruct(*v) for v in outs.values()],
-        in_specs=[hbm if k in ("w_gu", "w_dn") else vmem for k in args],
+        out_shape=[pltpu.VMEM(*v) for v in outs.values()],
+        in_specs=[hbm] * len(args),
         out_specs=[vmem] * len(outs),
         scratch_shapes=[pltpu.VMEM(*v) for v in scratch.values()]
         + [pltpu.SemaphoreType.DMA(v) for v in sems.values()],
         compiler_params=pltpu.CompilerParams(
-            collective_id=1, has_side_effects=True, vmem_limit_bytes=56 * 1024 * 1024
+            collective_id=1, has_side_effects=True, vmem_limit_bytes=LIMIT_RELAY * 1024 * 1024
         ),
     )(*args.values())
     made = types.SimpleNamespace(**dict(zip(outs, made)))

time: 127 us -> 120 us (0.945)
  Pallas kernels: 127 us -> 119 us
    pallas_call x1, Pallas kernels: 119 us -> 113 us  [local(): pl.pallas_call(functools.partial(relay_body, cfg, list(args) + list(outs)...]
    pallas_call x1, Pallas kernels: 7.37 us -> 5.89 us  [weight_grads(): pl.pallas_call(functools.partial(weight_body, WEIGHT_STEPS, len(others)),...]
where the time goes in v2:
time: 120 us
  Pallas kernels  119 us (99%)
    pallas_call x1, Pallas kernels, local(): pl.pallas_call(functools.partial(relay_body, cfg, list(args) + list(outs)...  113 us
    pallas_call x1, Pallas kernels, weight_grads(): pl.pallas_call(functools.partial(weight_body, WEIGHT_STEPS, len(others)),...  5.89 us

profile of v2, /device:TPU:0, one launch (start us, length us, event | category | flops | bytes accessed | tf_op | source)
XLA Modules:
  0.0 119.5 jit_solution(8019959180335867435)
XLA Ops:
  0.6 113.0 %shard_map.110 = (bf16[8,32,2048]{2,1,0:T(8,128)(2,1)S(1)}, bf16[8,32,1024]{2,1,0:T(8,128)(2,1)S(1)}, bf16[8,32,512]{2,1,0:T(8,128)(2,1)S(1)}, bf16[8,32,2048]{2...) custom-call(bf16[8,16,1024]{2,1,0:T(8,128)(2,1)} %refs_0_.1, ...), custom_call_target="tpu_custom_call" | custom-call | tf_op jit(solution)/shard_map/pallas_call | solution.py:560
  113.7 5.9 %shard_map.111 = (f32[2048,1024]{1,0:T(8,128)}, f32[512,2048]{1,0:T(8,128)}, bf16[8,16,1024]{2,1,0:T(8,128)(2,1)}, f32[16,2048]{1,0:T(8,128)}, f32[1,2048]{1,0:T(1,128)}) custom-call(bf16[256,2048]{1,0:T(8,128)(2,1)S(1)} %bitcast.17, bf16[256,1024]{1,0:T(8,128)(2,1)S(1)} %bitcast.19, bf16[256,512]{1,0:T(8,128)(2,1)S(1)} %bitcast.20, ...), custom_call_target="tpu_custom_call" | custom-call | tf_op jit(solution)/shard_map/pallas_call | solution.py:498

commit v3 on v2

--- a/solution.py
+++ b/solution.py
@@ -474,12 +474,10 @@
     grad_gu, grad_dn = refs[4 + n_other : 6 + n_other]
     kept = refs[6 + n_other : 6 + 2 * n_other]
     up, down, sem = refs[6 + 2 * n_other :]
-    for given, copy in zip(others, kept):
-        copy[...] = given[...]
     writes = []
     for i in range(steps):
         for k, (buf, out, left, right) in enumerate(
-            ((up, grad_gu, rows, q), (down, grad_dn, hidden, dy))
+            ((down, grad_dn, hidden, dy), (up, grad_gu, rows, q))
         ):
             size = buf.shape[0] // steps
             at = pl.ds(i * size, size)
@@ -487,6 +485,8 @@
             write = pltpu.make_async_copy(buf.at[at], out.at[at], sem.at[k, i])
             write.start()
             writes.append(write)
+    for given, copy in zip(others, kept):
+        copy[...] = given[...]
     for write in writes:
         write.wait()
 

time: 120 us -> 120 us (level)
  no operation moved by 1% of the time
where the time goes in v3:
time: 120 us; the launch traced here: 119 us
  Pallas kernels  119 us (99%)
    pallas_call x1, Pallas kernels, local(): pl.pallas_call(functools.partial(relay_body, cfg, list(args) + list(outs)...  113 us
    pallas_call x1, Pallas kernels, weight_grads(): pl.pallas_call(functools.partial(weight_body, WEIGHT_STEPS, len(others)),...  5.74 us

profile of v3, /device:TPU:0, one launch (start us, length us, event | category | flops | bytes accessed | tf_op | source)
XLA Modules:
  0.0 119.4 jit_solution(1467087913042780777)
XLA Ops:
  0.6 113.0 %shard_map.110 = (bf16[8,32,2048]{2,1,0:T(8,128)(2,1)S(1)}, bf16[8,32,1024]{2,1,0:T(8,128)(2,1)S(1)}, bf16[8,32,512]{2,1,0:T(8,128)(2,1)S(1)}, bf16[8,32,2048]{2...) custom-call(bf16[8,16,1024]{2,1,0:T(8,128)(2,1)} %refs_0_.1, ...), custom_call_target="tpu_custom_call" | custom-call | tf_op jit(solution)/shard_map/pallas_call | solution.py:560
  113.7 5.7 %shard_map.111 = (f32[2048,1024]{1,0:T(8,128)}, f32[512,2048]{1,0:T(8,128)}, bf16[8,16,1024]{2,1,0:T(8,128)(2,1)}, f32[16,2048]{1,0:T(8,128)}, f32[1,2048]{1,0:T(1,128)}) custom-call(bf16[256,2048]{1,0:T(8,128)(2,1)S(1)} %bitcast.17, bf16[256,1024]{1,0:T(8,128)(2,1)S(1)} %bitcast.19, bf16[256,512]{1,0:T(8,128)(2,1)S(1)} %bitcast.20, ...), custom_call_target="tpu_custom_call" | custom-call | tf_op jit(solution)/shard_map/pallas_call | solution.py:498
